TPU v7x, 32 devices: a whole 2x2x4 slice. The times are simulated.
32 devices in a mesh: section: 2 (over core), expert: 16 (over z, y, x).
Axes of the slice: x: 2, y: 2, z: 4, core: 2. Of those that a mesh axis runs over, the one named last changes fastest.
Arguments:
- act_in: bfloat16 [2, 2048, 7168], P('section', 'expert'), may hold values from -6 to 6
- cotangent: bfloat16 [2, 2048, 7168], P('section', 'expert'), may hold values from -6 to 6
- fwd_ids: int32 [2, 2048, 8], P('section', 'expert'), may hold values from 0 to 255, as said below
- fwd_gates: float32 [2, 2048, 8], P('section', 'expert'), may hold values from 0.05 to 0.8
- bwd_ids: int32 [2, 2048, 8], P('section', 'expert'), may hold values from 0 to 255, as said below
- bwd_gates: float32 [2, 2048, 8], P('section', 'expert'), may hold values from 0.05 to 0.8
- gate_w: bfloat16 [2, 7168, 2048], P('section', None, 'expert'), may hold values from -0.0625 to 0.0625
- up_w: bfloat16 [2, 7168, 2048], P('section', None, 'expert'), may hold values from -0.0625 to 0.0625
- down_w: bfloat16 [2, 2048, 7168], P('section', 'expert'), may hold values from -0.125 to 0.125
- gate_pre: bfloat16 [2, 160, 2048], P('section', None, 'expert'), may hold values from -6 to 6
- up_pre: bfloat16 [2, 160, 2048], P('section', None, 'expert'), may hold values from -6 to 6
Outputs:
- next_act: bfloat16 [2, 2048, 7168], P('section', 'expert')
- prev_grad: bfloat16 [2, 2048, 7168], P('section', 'expert')
- gate_grad: float32 [2, 2048, 8], P('section', 'expert')
Inputs may be any that keep to these rules, and one draw needn't show every extreme that they name: `fwd_ids`: the 8 ids of a row differ. In each aligned block of 128 rows (the rows of one device) each id below 1 is named by at most 10 rows; in every section one such id is named by exactly 10 rows in every block. `bwd_ids`: as for fwd_ids.
All inputs are finite; a program needn't handle non-finite values.
Results may differ from a plain program's by a relative error of at most 0.012.
Values may be sent and summed in bfloat16 or wider, within the bound.
A program may use at most 128 MiB of HBM per device.

v0:
```python
import jax
import jax.numpy as jnp
from jax import lax
from jax.sharding import PartitionSpec as P

FF = 2048


def from_partner(value, axis, apart):
    mask = 2**apart
    pairs = [(source, source ^ mask) for source in range(lax.axis_size(axis))]
    return lax.ppermute(value, axis, pairs)


def from_behind(value, axis, steps):
    count = lax.axis_size(axis)
    pairs = [(source, (source + steps) % count) for source in range(count)]
    return lax.ppermute(value, axis, pairs)


def routing(ids, gates, experts, capacity):
    expert_ids = jnp.arange(experts, dtype=jnp.int32)
    matches = ids[None, :, :] == expert_ids[:, None, None]
    routed = jnp.any(matches, axis=2)
    weights = jnp.sum(jnp.where(matches, gates[None, :, :], 0.0), axis=2)
    position = jnp.cumsum(routed.astype(jnp.int32), axis=1) - 1
    slot_ids = jnp.arange(capacity, dtype=jnp.int32)
    placing = (position[:, None, :] == slot_ids[None, :, None]) & routed[:, None, :]
    return (matches, placing.astype(jnp.float32), weights)


def send_rows(tokens, placing):
    buffer = jnp.einsum(
        "ect,td->ecd", placing.astype(jnp.bfloat16), tokens, preferred_element_type=jnp.float32
    ).astype(jnp.bfloat16)
    experts, capacity, width = buffer.shape
    ndev = lax.axis_size("expert")
    slices = ndev // experts
    piece_width = width // slices
    pieces = buffer.reshape(experts, capacity, slices, piece_width).transpose(0, 2, 1, 3)
    pieces = pieces.reshape(ndev, capacity, piece_width)
    received = lax.all_to_all(pieces, "expert", split_axis=0, concat_axis=0, tiled=True)
    my_index = lax.axis_index("expert")
    for level in range(slices.bit_length() - 1):
        partner = from_partner(received, "expert", level)
        upper_side = my_index >> level & 1 == 1
        received = jnp.where(
            upper_side,
            jnp.concatenate([partner, received], axis=2),
            jnp.concatenate([received, partner], axis=2),
        )
    return received.reshape(ndev * capacity, width)


def split_halves(totals, level, my_index):
    half = totals.shape[2] // 2
    lower_half = totals[:, :, :half]
    upper_half = totals[:, :, half:]
    upper_side = my_index >> level & 1 == 1
    kept_half = jnp.where(upper_side, upper_half, lower_half)
    sent_half = jnp.where(upper_side, lower_half, upper_half)
    return (kept_half, sent_half)


def return_sums(partial_value, experts, capacity):
    ndev = lax.axis_size("expert")
    slices = ndev // experts
    width = partial_value.shape[1]
    rounded = partial_value.astype(jnp.bfloat16)
    totals = lax.optimization_barrier(rounded).astype(jnp.float32).reshape(ndev, capacity, width)
    my_index = lax.axis_index("expert")
    for level in reversed(range(slices.bit_length() - 1)):
        kept_half, sent_half = split_halves(totals, level, my_index)
        totals = kept_half + from_partner(sent_half.astype(jnp.bfloat16), "expert", level).astype(
            sent_half.dtype
        )
    back = lax.all_to_all(
        totals.astype(jnp.bfloat16), "expert", split_axis=0, concat_axis=0, tiled=True
    ).astype(totals.dtype)
    back = back.reshape(experts, slices, capacity, width // slices).transpose(0, 2, 1, 3)
    return back.reshape(experts, capacity, width)


def return_grads(partial_value, dots, experts, capacity):
    ndev = lax.axis_size("expert")
    slices = ndev // experts
    width = partial_value.shape[1]
    rounded = partial_value.astype(jnp.bfloat16)
    dots_rounded = dots.astype(jnp.bfloat16)
    kept_rows, kept_dots = lax.optimization_barrier((rounded, dots_rounded))
    totals = kept_rows.astype(jnp.float32).reshape(ndev, capacity, width)
    dot_totals = kept_dots.astype(jnp.float32).reshape(ndev, capacity)
    my_index = lax.axis_index("expert")
    for level in reversed(range(slices.bit_length() - 1)):
        kept_half, sent_half = split_halves(totals, level, my_index)
        got_half, got_dots = (
            from_partner(sent_half.astype(jnp.bfloat16), "expert", level).astype(sent_half.dtype),
            from_partner(dot_totals.astype(jnp.bfloat16), "expert", level).astype(dot_totals.dtype),
        )
        totals = kept_half + got_half
        dot_totals = dot_totals + got_dots
    back, back_dots = (
        lax.all_to_all(
            totals.astype(jnp.bfloat16), "expert", split_axis=0, concat_axis=0, tiled=True
        ).astype(totals.dtype),
        lax.all_to_all(
            dot_totals.astype(jnp.bfloat16), "expert", split_axis=0, concat_axis=0, tiled=True
        ).astype(dot_totals.dtype),
    )
    back = back.reshape(experts, slices, capacity, width // slices).transpose(0, 2, 1, 3)
    return (
        back.reshape(experts, capacity, width),
        back_dots.reshape(experts, slices, capacity)[:, 0],
    )


def body(
    act_in,
    cotangent,
    fwd_ids,
    fwd_gates,
    bwd_ids,
    bwd_gates,
    gate_w,
    up_w,
    down_w,
    gate_pre,
    up_pre,
):
    ndev = lax.axis_size("expert")
    w_gate = gate_w[0]
    w_up = up_w[0]
    w_down = down_w[0]
    ff_dev = w_gate.shape[1]
    slices = FF // ff_dev
    experts = ndev // slices
    capacity = gate_pre.shape[1] // ndev
    matches_f, placing_f, weights_f = routing(fwd_ids[0], fwd_gates[0], experts, capacity)
    slot_rows = send_rows(act_in[0], placing_f)
    gate_act = jnp.dot(slot_rows, w_gate, preferred_element_type=jnp.float32)
    up_act = jnp.dot(slot_rows, w_up, preferred_element_type=jnp.float32)
    hidden = (jax.nn.silu(gate_act) * up_act).astype(jnp.bfloat16)
    expert_out = return_sums(
        jnp.dot(hidden, w_down, preferred_element_type=jnp.float32), experts, capacity
    )
    mixed = jnp.einsum(
        "ect,ecd->td",
        placing_f * weights_f[:, None, :],
        expert_out,
        precision=lax.Precision.HIGHEST,
    )
    matches_b, placing_b, weights_b = routing(bwd_ids[0], bwd_gates[0], experts, capacity)
    grad_rows = send_rows(cotangent[0], placing_b)
    saved_gate = gate_pre[0].astype(jnp.float32)
    saved_up = up_pre[0].astype(jnp.float32)
    grad_hidden = jnp.einsum("rd,fd->rf", grad_rows, w_down, preferred_element_type=jnp.float32)
    sigmoid_gate = jax.nn.sigmoid(saved_gate)
    activated = saved_gate * sigmoid_gate
    gate_dots = jnp.sum(grad_hidden * activated * saved_up, axis=1)
    grad_gate_act = (
        grad_hidden * saved_up * sigmoid_gate * (1.0 + saved_gate * (1.0 - sigmoid_gate))
    ).astype(jnp.bfloat16)
    grad_up_act = (grad_hidden * activated).astype(jnp.bfloat16)
    grad_partial = jnp.einsum(
        "rf,df->rd", grad_gate_act, w_gate, preferred_element_type=jnp.float32
    )
    grad_partial = grad_partial + jnp.einsum(
        "rf,df->rd", grad_up_act, w_up, preferred_element_type=jnp.float32
    )
    expert_grad, expert_dots = return_grads(grad_partial, gate_dots, experts, capacity)
    input_grad = jnp.einsum(
        "ect,ecd->td",
        placing_b * weights_b[:, None, :],
        expert_grad,
        precision=lax.Precision.HIGHEST,
    )
    token_dots = jnp.einsum("ect,ec->et", placing_b, expert_dots, precision=lax.Precision.HIGHEST)
    gate_grad = jnp.sum(jnp.where(matches_b, token_dots[:, :, None], 0.0), axis=0)
    next_act = from_behind(mixed.astype(jnp.bfloat16)[None], "section", 1)
    prev_grad = from_behind(input_grad.astype(jnp.bfloat16)[None], "section", -1)
    return (next_act, prev_grad, gate_grad[None])


def solution(mesh):
    in_specs = (
        P("section", "expert", None),
        P("section", "expert", None),
        P("section", "expert", None),
        P("section", "expert", None),
        P("section", "expert", None),
        P("section", "expert", None),
        P("section", None, "expert"),
        P("section", None, "expert"),
        P("section", "expert", None),
        P("section", None, "expert"),
        P("section", None, "expert"),
    )
    out_specs = (
        P("section", "expert", None),
        P("section", "expert", None),
        P("section", "expert", None),
    )
    return jax.shard_map(body, mesh=mesh, in_specs=in_specs, out_specs=out_specs, check_vma=False)
```

profile of v0, /device:TPU:0, one launch (start us, length us, event | category | flops | bytes accessed | tf_op | source)
XLA Modules:
  0.0 370.6 jit_solution(8726770225497989146)
XLA Ops:
  1.9 1.9 convolution_convert_fusion.4
  4.8 8.3 %all-to-all-start = ((bf16[16,10,448]{2,1,0:T(8,128)(2,1)}), bf16[16,10,448]{2,1,0:T(8,128)(2,1)S(1)}, u32[]{:S(2)}, u32[]{:S(2)}) async-start(bf16[16,10,448]{2,1,0:T(8,128)(2,1)} %bitcast.86), calls=%async_computation | async-start | bytes 524288 | tf_op jit(solution)/shard_map/all_to_all | solution.py:42
  13.6 1.9 convolution_convert_fusion.3
  16.5 6.5 %all-to-all-done = bf16[16,10,448]{2,1,0:T(8,128)(2,1)S(1)} async-done(((bf16[16,10,448]{2,1,0:T(8,128)(2,1)}), bf16[16,10,448]{2,1,0:T(8,128)(2,1)S(1)}, u32[]{:S(2)}, u32[]{:S(2)}) %all-to-all-start) | async-done | bytes 143392 | tf_op jit(solution)/shard_map/all_to_all | solution.py:42
  23.1 3.5 all-to-all-start.2
  26.6 1.9 collective-permute-start
  28.5 7.3 %all-to-all-done.2 = bf16[16,10,448]{2,1,0:T(8,128)(2,1)S(1)} async-done(((bf16[16,10,448]{2,1,0:T(8,128)(2,1)}), bf16[16,10,448]{2,1,0:T(8,128)(2,1)S(1)}, u32[]{:S(2)}, u32[]{:S(2)}) %all-to-all-start.2) | async-done | bytes 143392 | tf_op jit(solution)/shard_map/all_to_all | solution.py:42
  39.2 1.5 collective-permute-start.1
  40.7 1.6 collective-permute-done.9
  42.6 1.5 collective-permute-start.10
  44.3 1.9 maximum_select_fusion.15
  47.1 5.8 %collective-permute-done.1 = bf16[16,10,896]{2,1,0:T(8,128)(2,1)} collective-permute-done((bf16[16,10,896]{2,1,0:T(8,128)(2,1)}, bf16[16,10,896]{2,1,0:T(8,128)(2,1)}, u32[]{:S(2)}, u32[]{:S(2)}) %collective-permute-start.1) | collective-permute-done | bytes 286752 | tf_op jit(solution)/shard_map/ppermute | solution.py:12
  52.9 1.7 maximum_select_fusion.7
  55.8 1.5 collective-permute-start.2
  57.3 2.0 collective-permute-done.10
  59.3 1.4 maximum_select_fusion.8
  62.6 1.8 concatenate.116
  64.5 1.8 concatenate.135
  66.3 1.4 maximum_select_fusion.9
  67.7 2.2 maximum_select_fusion.10
  72.7 1.7 copy.120
  74.3 2.0 collective-permute-start.3
  76.3 7.1 %collective-permute-done.11 = bf16[16,10,1792]{2,0,1:T(8,128)(2,1)} collective-permute-done((bf16[16,10,1792]{2,0,1:T(8,128)(2,1)}, bf16[16,10,1792]{2,0,1:T(8,128)(2,1)}, u32[]{:S(2)}, u32[]{:S(2)}) %collective-permute-start.11) | collective-permute-done | bytes 573472 | tf_op jit(solution)/shard_map/ppermute | solution.py:12
  85.6 1.8 maximum_select_fusion.4
  87.4 2.2 concatenate.115
  90.6 3.2 copy.132
  96.4 55.0 %collective-permute-done.3 = bf16[16,10,3584]{2,0,1:T(8,128)(2,1)} collective-permute-done((bf16[16,10,3584]{2,0,1:T(8,128)(2,1)}, bf16[16,10,3584]{2,0,1:T(8,128)(2,1)}, u32[]{:S(2)}, u32[]{:S(2)}) %collective-permute-start.3) | collective-permute-done | bytes 1146912 | tf_op jit(solution)/shard_map/ppermute | solution.py:12
  151.4 3.2 copy.121
  154.6 2.6 concatenate.114
  157.1 3.0 fusion.14
  160.2 5.2 %convolution_convert_fusion = bf16[160,7168]{1,0:T(8,128)(2,1)} fusion(bf16[1,128,7168]{2,1,0:T(8,128)(2,1)} %param.19, f32[160,128]{1,0:T(8,128)S(1)} %fusion.14, bf16[1,7168,128]{2,1,0:T(8,128)(2,1)S(1)} %copy-done, bf16[160,3584]{1,0:T(8,128)(2,1)S(1)} %copy-done.15, bf16[160,3584]{1,0:T(8,128)(2,1)} %concatenate.114, pred[]{:T(512)S(6)} %eq.80), kind=kOutput, calls=%fused_computation.2 | convolution fusion | flops 598794240 | bytes 8339457 | tf_op jit(solution)/shard_map/dot_general | solution.py:144
  165.3 5.2 %reshape.366 = f32[16,10,7168]{2,1,0:T(8,128)} reshape(bf16[160,7168]{1,0:T(8,128)(2,1)} %convolution_convert_fusion) | data formatting | bytes 6881280 | tf_op jit(solution)/shard_map/reshape | solution.py:70
  170.5 3.9 %fusion.75 = (f32[16,10,3584]{2,1,0:T(8,128)S(1)}, f32[16,10,3584]{2,1,0:T(8,128)S(1)}) fusion(f32[16,10,7168]{2,1,0:T(8,128)} %reshape.366), kind=kLoop, calls=%fused_computation.129 | loop fusion | bytes 9175040 | tf_op jit(solution)/shard_map/slice | solution.py:58
  174.5 2.4 select_convert_fusion.1
  177.5 3.2 copy.133
  180.6 2.5 concatenate.133
  183.1 3.8 %fusion.24 = (bf16[160]{0:T(256)(128)(2,1)S(1)}, f32[160,128]{1,0:T(8,128)S(1)}) fusion(bf16[1,160,128]{2,1,0:T(8,128)(2,1)S(1)} %copy-done.18, bf16[1,160,128]{2,1,0:T(8,128)(2,1)S(1)} %copy-done.17, bf16[1,128,7168]{2,1,0:T(8,128)(2,1)} %param.19, bf16[160,3584]{1,0:T(8,128)(2,1)} %maximum_select_fusion.6, bf16[160,3584]{1,0:T(8,128)(2,1)} %concatenate.133, ...), kind=kOutput, calls=%fused_computation.68 | convolution fusion | flops 304107360 | bytes 4292929 | tf_op jit(solution)/shard_map/rd,fd->rf/dot_general | solution.py:156
  188.4 2.1 fusion
  190.5 5.2 %reshape.371 = f32[16,10,7168]{2,1,0:T(8,128)} reshape(bf16[160,7168]{1,0:T(8,128)(2,1)} %fusion) | data formatting | bytes 6881280 | tf_op jit(solution)/shard_map/reshape | solution.py:91
  195.7 3.9 %fusion.74 = (f32[16,10,3584]{2,1,0:T(8,128)S(1)}, f32[16,10,3584]{2,1,0:T(8,128)S(1)}) fusion(f32[16,10,7168]{2,1,0:T(8,128)} %reshape.371), kind=kLoop, calls=%fused_computation.128 | loop fusion | bytes 9175040 | tf_op jit(solution)/shard_map/slice | solution.py:58
  199.7 2.4 select_convert_fusion
  202.1 3.0 collective-permute-start.13
  205.1 45.3 %collective-permute-done.4 = bf16[16,10,3584]{2,0,1:T(8,128)(2,1)} collective-permute-done((bf16[16,10,3584]{2,0,1:T(8,128)(2,1)S(1)}, bf16[16,10,3584]{2,0,1:T(8,128)(2,1)}, u32[]{:S(2)}, u32[]{:S(2)}) %collective-permute-start.4) | collective-permute-done | bytes 1146912 | tf_op jit(solution)/shard_map/ppermute | solution.py:12
  250.5 3.8 %convert_add_fusion.1 = f32[16,10,3584]{2,0,1:T(8,128)S(1)} fusion(bf16[16,10,3584]{2,0,1:T(8,128)(2,1)} %collective-permute-done.4, f32[16,10,3584]{2,1,0:T(8,128)S(1)} %copy-done.5, f32[16,10,3584]{2,1,0:T(8,128)S(1)} %copy-done.3, pred[]{:T(512)S(6)} %eq.80), kind=kLoop, calls=%fused_computation.19 | loop fusion | flops 1720320 | bytes 8028161 | tf_op jit(solution)/shard_map/add | solution.py:74
  254.5 18.0 %collective-permute-done.13 = bf16[16,10,3584]{2,0,1:T(8,128)(2,1)S(1)} collective-permute-done((bf16[16,10,3584]{2,0,1:T(8,128)(2,1)S(1)}, bf16[16,10,3584]{2,0,1:T(8,128)(2,1)S(1)}, u32[]{:S(2)}, u32[]{:S(2)}) %collective-permute-start.13) | collective-permute-done | bytes 1146912 | tf_op jit(solution)/shard_map/ppermute | solution.py:12
  272.5 2.6 convert_add_fusion
  275.2 9.5 %collective-permute-done.5 = bf16[16,10,1792]{2,0,1:T(8,128)(2,1)S(1)} collective-permute-done((bf16[16,10,1792]{2,0,1:T(8,128)(2,1)S(1)}, bf16[16,10,1792]{2,0,1:T(8,128)(2,1)S(1)}, u32[]{:S(2)}, u32[]{:S(2)}) %collective-permute-start.5) | collective-permute-done | bytes 573472 | tf_op jit(solution)/shard_map/ppermute | solution.py:12
  286.4 10.6 %collective-permute-done.14 = bf16[16,10,1792]{2,0,1:T(8,128)(2,1)S(1)} collective-permute-done((bf16[16,10,1792]{2,0,1:T(8,128)(2,1)S(1)}, bf16[16,10,1792]{2,0,1:T(8,128)(2,1)S(1)}, u32[]{:S(2)}, u32[]{:S(2)}) %collective-permute-start.14) | collective-permute-done | bytes 573472 | tf_op jit(solution)/shard_map/ppermute | solution.py:12
  298.8 2.2 collective-permute-start.7
  301.0 5.0 %collective-permute-done.15 = bf16[16,10,896]{2,0,1:T(8,128)(2,1)S(1)} collective-permute-done((bf16[16,10,896]{2,0,1:T(8,128)(2,1)S(1)}, bf16[16,10,896]{2,0,1:T(8,128)(2,1)S(1)}, u32[]{:S(2)}, u32[]{:S(2)}) %collective-permute-start.15) | collective-permute-done | bytes 286752 | tf_op jit(solution)/shard_map/ppermute | solution.py:12
  306.2 1.8 collective-permute-start.16
  309.0 3.7 %all-to-all-start.1 = ((bf16[16,10,448]{2,1,0:T(8,128)(2,1)}), bf16[16,10,448]{2,1,0:T(8,128)(2,1)S(1)}, u32[]{:S(2)}, u32[]{:S(2)}) async-start(bf16[16,10,448]{2,1,0:T(8,128)(2,1)} %copy.125), calls=%async_computation.1 | async-start | bytes 524288 | tf_op jit(solution)/shard_map/all_to_all | solution.py:77
  313.7 8.2 %all-to-all-done.1 = bf16[16,10,448]{2,1,0:T(8,128)(2,1)S(1)} async-done(((bf16[16,10,448]{2,1,0:T(8,128)(2,1)}), bf16[16,10,448]{2,1,0:T(8,128)(2,1)S(1)}, u32[]{:S(2)}, u32[]{:S(2)}) %all-to-all-start.1) | async-done | bytes 143392 | tf_op jit(solution)/shard_map/all_to_all | solution.py:77
  322.0 3.8 %all-to-all-start.3 = ((bf16[16,10,448]{2,1,0:T(8,128)(2,1)}), bf16[16,10,448]{2,1,0:T(8,128)(2,1)S(1)}, u32[]{:S(2)}, u32[]{:S(2)}) async-start(bf16[16,10,448]{2,1,0:T(8,128)(2,1)} %copy.137), calls=%async_computation.3 | async-start | bytes 524288 | tf_op jit(solution)/shard_map/all_to_all | solution.py:103
  326.1 1.6 fusion.1
  327.8 6.8 %all-to-all-done.3 = bf16[16,10,448]{2,1,0:T(8,128)(2,1)S(1)} async-done(((bf16[16,10,448]{2,1,0:T(8,128)(2,1)}), bf16[16,10,448]{2,1,0:T(8,128)(2,1)S(1)}, u32[]{:S(2)}, u32[]{:S(2)}) %all-to-all-start.3) | async-done | bytes 143392 | tf_op jit(solution)/shard_map/all_to_all | solution.py:103
  334.9 2.9 fusion.2
  338.7 3.8 %collective-permute-done.18 = bf16[16,10]{1,0:T(8,128)(2,1)S(1)} collective-permute-done((bf16[16,10]{1,0:T(8,128)(2,1)S(1)}, bf16[16,10]{1,0:T(8,128)(2,1)S(1)}, u32[]{:S(2)}, u32[]{:S(2)}) %collective-permute-start.18) | collective-permute-done | bytes 352 | tf_op jit(solution)/shard_map/ppermute | solution.py:12
  343.6 2.5 collective-permute-done.19
  347.0 2.7 collective-permute-done.20
  350.5 2.8 collective-permute-done.21
  353.3 10.6 %all_to_all.29 = bf16[16,1,10]{2,1,0:T(2,128)(2,1)S(1)} all-to-all(bf16[16,1,10]{2,1,0:T(2,128)(2,1)S(1)} %copy.139), channel_id=1, replica_groups=mesh['section'=2,'expert'=16] {'expert'}, dimensions={0} | all-to-all | bytes 640 | tf_op jit(solution)/shard_map/all_to_all | solution.py:106
  364.7 3.0 copy.161
  367.7 2.8 copy.162
  (123 shorter events, 33.1 us)
Async XLA Ops:
  0.6 159.5 %copy-start = (bf16[1,7168,128]{2,1,0:T(8,128)(2,1)S(1)}, bf16[1,7168,128]{2,1,0:T(8,128)(2,1)}, u32[]{:S(2)}) copy-start(bf16[1,7168,128]{2,1,0:T(8,128)(2,1)} %param.17) | copy-start | bytes 5505028
  1.5 11.7 %copy-start.19 = (f32[1,128,8]{1,2,0:T(8,128)S(1)}, f32[1,128,8]{1,2,0:T(8,128)}, u32[]{:S(2)}) copy-start(f32[1,128,8]{1,2,0:T(8,128)} %param.16) | copy-start | bytes 12292
  1.5 11.7 %copy-start.20 = (s32[1,128,8]{1,2,0:T(8,128)S(1)}, s32[1,128,8]{1,2,0:T(8,128)}, u32[]{:S(2)}) copy-start(s32[1,128,8]{1,2,0:T(8,128)} %param.15) | copy-start | bytes 12292
  4.8 18.2 %all-to-all-start = ((bf16[16,10,448]{2,1,0:T(8,128)(2,1)}), bf16[16,10,448]{2,1,0:T(8,128)(2,1)S(1)}, u32[]{:S(2)}, u32[]{:S(2)}) async-start(bf16[16,10,448]{2,1,0:T(8,128)(2,1)} %bitcast.86), calls=%async_computation | async-start | bytes 524288 | tf_op jit(solution)/shard_map/all_to_all | solution.py:42
  23.1 12.8 %all-to-all-start.2 = ((bf16[16,10,448]{2,1,0:T(8,128)(2,1)}), bf16[16,10,448]{2,1,0:T(8,128)(2,1)S(1)}, u32[]{:S(2)}, u32[]{:S(2)}) async-start(bf16[16,10,448]{2,1,0:T(8,128)(2,1)} %bitcast.85), calls=%async_computation.2 | async-start | bytes 524288 | tf_op jit(solution)/shard_map/all_to_all | solution.py:42
  26.6 11.5 %collective-permute-start = (bf16[16,10,448]{2,1,0:T(8,128)(2,1)S(1)}, bf16[16,10,448]{2,1,0:T(8,128)(2,1)S(1)}, u32[]{:S(2)}, u32[]{:S(2)}) collective-permute-start(bf16[16,10,448]{2,1,0:T(8,128)(2,1)S(1)} %all-to-all-done), channel_id=1, source_target_pairs={{0,1},{1,0},{2,3},{3,2},{4,5},{5,4},{6,7},{7,6},{8,9},{9,8},{10,11... | collective-permute-start | bytes 430088 | tf_op jit(solution)/shard_map/ppermute | solution.py:12
  35.9 6.4 %collective-permute-start.9 = (bf16[16,10,448]{2,1,0:T(8,128)(2,1)S(1)}, bf16[16,10,448]{2,1,0:T(8,128)(2,1)S(1)}, u32[]{:S(2)}, u32[]{:S(2)}) collective-permute-start(bf16[16,10,448]{2,1,0:T(8,128)(2,1)S(1)} %all-to-all-done.2), channel_id=1, source_target_pairs={{0,1},{1,0},{2,3},{3,2},{4,5},{5,4},{6,7},{7,6},{8,9},{9,8},{10,11... | collective-permute-start | bytes 430088 | tf_op jit(solution)/shard_map/ppermute | solution.py:12
  39.2 7.0 %copy-start.16 = (bf16[160,448]{1,0:T(8,128)(2,1)S(1)}, bf16[160,448]{1,0:T(8,128)(2,1)}, u32[]{:S(2)}) copy-start(bf16[160,448]{1,0:T(8,128)(2,1)} %concatenate.137) | copy-start | bytes 430084
  39.2 13.7 %collective-permute-start.1 = (bf16[16,10,896]{2,1,0:T(8,128)(2,1)}, bf16[16,10,896]{2,1,0:T(8,128)(2,1)}, u32[]{:S(2)}, u32[]{:S(2)}) collective-permute-start(bf16[16,10,896]{2,1,0:T(8,128)(2,1)} %maximum_select_fusion.11), channel_id=1, source_target_pairs={{0,2},{1,3},{2,0},{3,1},{4,6},{5,7},{6,4},{7,5},{8,10},{9,11},{10,... | collective-permute-start | bytes 860168 | tf_op jit(solution)/shard_map/ppermute | solution.py:12
  42.6 16.7 %collective-permute-start.10 = (bf16[16,10,896]{2,1,0:T(8,128)(2,1)S(1)}, bf16[16,10,896]{2,1,0:T(8,128)(2,1)}, u32[]{:S(2)}, u32[]{:S(2)}) collective-permute-start(bf16[16,10,896]{2,1,0:T(8,128)(2,1)S(1)} %maximum_select_fusion.12), channel_id=1, source_target_pairs={{0,2},{1,3},{2,0},{3,1},{4,6},{5,7},{6,4},{7,5},{8,10},{9,11},{10,... | collective-permute-start | bytes 860168 | tf_op jit(solution)/shard_map/ppermute | solution.py:12
  54.7 7.1 %copy-start.6 = (bf16[16,10,1792]{2,1,0:T(8,128)(2,1)}, bf16[16,10,1792]{2,1,0:T(8,128)(2,1)S(1)}, u32[]{:S(2)}) copy-start(bf16[16,10,1792]{2,1,0:T(8,128)(2,1)S(1)} %maximum_select_fusion.7) | copy-start | bytes 1720324
  55.8 14.7 %collective-permute-start.2 = (bf16[16,10,1792]{2,0,1:T(8,128)(2,1)}, bf16[16,10,1792]{2,0,1:T(8,128)(2,1)}, u32[]{:S(2)}, u32[]{:S(2)}) collective-permute-start(bf16[16,10,1792]{2,0,1:T(8,128)(2,1)} %copy.117), channel_id=1, source_target_pairs={{0,4},{1,5},{2,6},{3,7},{4,0},{5,1},{6,2},{7,3},{8,12},{9,13},{10,... | collective-permute-start | bytes 1720328 | tf_op jit(solution)/shard_map/ppermute | solution.py:12
  61.7 21.7 %collective-permute-start.11 = (bf16[16,10,1792]{2,0,1:T(8,128)(2,1)}, bf16[16,10,1792]{2,0,1:T(8,128)(2,1)}, u32[]{:S(2)}, u32[]{:S(2)}) collective-permute-start(bf16[16,10,1792]{2,0,1:T(8,128)(2,1)} %copy.129), channel_id=1, source_target_pairs={{0,4},{1,5},{2,6},{3,7},{4,0},{5,1},{6,2},{7,3},{8,12},{9,13},{10,... | collective-permute-start | bytes 1720328 | tf_op jit(solution)/shard_map/ppermute | solution.py:12
  66.3 5.4 %copy-start.7 = (bf16[16,10,1792]{2,1,0:T(8,128)(2,1)S(1)}, bf16[16,10,1792]{2,1,0:T(8,128)(2,1)}, u32[]{:S(2)}) copy-start(bf16[16,10,1792]{2,1,0:T(8,128)(2,1)} %copy-done.6) | copy-start | bytes 1720324
  71.7 0.9 copy-start.8
  74.3 77.1 %collective-permute-start.3 = (bf16[16,10,3584]{2,0,1:T(8,128)(2,1)}, bf16[16,10,3584]{2,0,1:T(8,128)(2,1)}, u32[]{:S(2)}, u32[]{:S(2)}) collective-permute-start(bf16[16,10,3584]{2,0,1:T(8,128)(2,1)} %copy.120), channel_id=1, source_target_pairs={{0,8},{1,9},{2,10},{3,11},{4,12},{5,13},{6,14},{7,15},{8,0},{9,1},... | collective-permute-start | bytes 3440648 | tf_op jit(solution)/shard_map/ppermute | solution.py:12
  84.7 0.9 copy-start.9
  87.4 2.2 copy-start.10
  90.6 3.2 copy-start.13
  93.8 1.3 copy-start.11
  93.8 1.3 copy-start.12
  93.8 83.7 %collective-permute-start.12 = (bf16[16,10,3584]{2,0,1:T(8,128)(2,1)}, bf16[16,10,3584]{2,0,1:T(8,128)(2,1)}, u32[]{:S(2)}, u32[]{:S(2)}) collective-permute-start(bf16[16,10,3584]{2,0,1:T(8,128)(2,1)} %copy.132), channel_id=1, source_target_pairs={{0,8},{1,9},{2,10},{3,11},{4,12},{5,13},{6,14},{7,15},{8,0},{9,1},... | collective-permute-start | bytes 3440648 | tf_op jit(solution)/shard_map/ppermute | solution.py:12
  154.6 2.6 copy-start.15
  174.5 2.5 copy-start.2
  174.5 3.0 copy-start.4
  177.5 73.0 %collective-permute-start.4 = (bf16[16,10,3584]{2,0,1:T(8,128)(2,1)S(1)}, bf16[16,10,3584]{2,0,1:T(8,128)(2,1)}, u32[]{:S(2)}, u32[]{:S(2)}) collective-permute-start(bf16[16,10,3584]{2,0,1:T(8,128)(2,1)S(1)} %select_convert_fusion.1), channel_id=1, source_target_pairs={{0,8},{1,9},{2,10},{3,11},{4,12},{5,13},{6,14},{7,15},{8,0},{9,1},... | collective-permute-start | bytes 3440648 | tf_op jit(solution)/shard_map/ppermute | solution.py:12
  180.6 2.5 copy-start.17
  180.6 2.5 copy-start.18
  186.9 1.5 copy-start.14
  199.7 50.8 %copy-start.3 = (f32[16,10,3584]{2,1,0:T(8,128)S(1)}, f32[16,10,3584]{2,1,0:T(8,128)}, u32[]{:S(2)}) copy-start(f32[16,10,3584]{2,1,0:T(8,128)} %copy-done.2) | copy-start | bytes 6881284
  199.7 50.8 %copy-start.5 = (f32[16,10,3584]{2,1,0:T(8,128)S(1)}, f32[16,10,3584]{2,1,0:T(8,128)}, u32[]{:S(2)}) copy-start(f32[16,10,3584]{2,1,0:T(8,128)} %copy-done.4) | copy-start | bytes 6881284
  202.1 70.4 %collective-permute-start.13 = (bf16[16,10,3584]{2,0,1:T(8,128)(2,1)S(1)}, bf16[16,10,3584]{2,0,1:T(8,128)(2,1)S(1)}, u32[]{:S(2)}, u32[]{:S(2)}) collective-permute-start(bf16[16,10,3584]{2,0,1:T(8,128)(2,1)S(1)} %select_convert_fusion), channel_id=1, source_target_pairs={{0,8},{1,9},{2,10},{3,11},{4,12},{5,13},{6,14},{7,15},{8,0},{9,1},... | collective-permute-start | bytes 3440648 | tf_op jit(solution)/shard_map/ppermute | solution.py:12
  254.4 30.4 %collective-permute-start.5 = (bf16[16,10,1792]{2,0,1:T(8,128)(2,1)S(1)}, bf16[16,10,1792]{2,0,1:T(8,128)(2,1)S(1)}, u32[]{:S(2)}, u32[]{:S(2)}) collective-permute-start(bf16[16,10,1792]{2,0,1:T(8,128)(2,1)S(1)} %select_convert_fusion.3), channel_id=1, source_target_pairs={{0,4},{1,5},{2,6},{3,7},{4,0},{5,1},{6,2},{7,3},{8,12},{9,13},{10,... | collective-permute-start | bytes 1720328 | tf_op jit(solution)/shard_map/ppermute | solution.py:12
  275.2 21.8 %collective-permute-start.14 = (bf16[16,10,1792]{2,0,1:T(8,128)(2,1)S(1)}, bf16[16,10,1792]{2,0,1:T(8,128)(2,1)S(1)}, u32[]{:S(2)}, u32[]{:S(2)}) collective-permute-start(bf16[16,10,1792]{2,0,1:T(8,128)(2,1)S(1)} %select_convert_fusion.2), channel_id=1, source_target_pairs={{0,4},{1,5},{2,6},{3,7},{4,0},{5,1},{6,2},{7,3},{8,12},{9,13},{10,... | collective-permute-start | bytes 1720328 | tf_op jit(solution)/shard_map/ppermute | solution.py:12
  285.0 13.6 %collective-permute-start.6 = (bf16[16,10,896]{2,0,1:T(8,128)(2,1)S(1)}, bf16[16,10,896]{2,0,1:T(8,128)(2,1)S(1)}, u32[]{:S(2)}, u32[]{:S(2)}) collective-permute-start(bf16[16,10,896]{2,0,1:T(8,128)(2,1)S(1)} %select_convert_fusion.5), channel_id=1, source_target_pairs={{0,2},{1,3},{2,0},{3,1},{4,6},{5,7},{6,4},{7,5},{8,10},{9,11},{10,... | collective-permute-start | bytes 860168 | tf_op jit(solution)/shard_map/ppermute | solution.py:12
  297.2 8.8 %collective-permute-start.15 = (bf16[16,10,896]{2,0,1:T(8,128)(2,1)S(1)}, bf16[16,10,896]{2,0,1:T(8,128)(2,1)S(1)}, u32[]{:S(2)}, u32[]{:S(2)}) collective-permute-start(bf16[16,10,896]{2,0,1:T(8,128)(2,1)S(1)} %select_convert_fusion.4), channel_id=1, source_target_pairs={{0,2},{1,3},{2,0},{3,1},{4,6},{5,7},{6,4},{7,5},{8,10},{9,11},{10,... | collective-permute-start | bytes 860168 | tf_op jit(solution)/shard_map/ppermute | solution.py:12
  298.8 9.2 %collective-permute-start.7 = (bf16[16,10,448]{2,0,1:T(8,128)(2,1)S(1)}, bf16[16,10,448]{2,0,1:T(8,128)(2,1)S(1)}, u32[]{:S(2)}, u32[]{:S(2)}) collective-permute-start(bf16[16,10,448]{2,0,1:T(8,128)(2,1)S(1)} %select_convert_fusion.7), channel_id=1, source_target_pairs={{0,1},{1,0},{2,3},{3,2},{4,5},{5,4},{6,7},{7,6},{8,9},{9,8},{10,11... | collective-permute-start | bytes 430088 | tf_op jit(solution)/shard_map/ppermute | solution.py:12
  306.2 6.6 %collective-permute-start.16 = (bf16[16,10,448]{2,0,1:T(8,128)(2,1)S(1)}, bf16[16,10,448]{2,0,1:T(8,128)(2,1)S(1)}, u32[]{:S(2)}, u32[]{:S(2)}) collective-permute-start(bf16[16,10,448]{2,0,1:T(8,128)(2,1)S(1)} %select_convert_fusion.6), channel_id=1, source_target_pairs={{0,1},{1,0},{2,3},{3,2},{4,5},{5,4},{6,7},{7,6},{8,9},{9,8},{10,11... | collective-permute-start | bytes 430088 | tf_op jit(solution)/shard_map/ppermute | solution.py:12
  309.0 13.0 %all-to-all-start.1 = ((bf16[16,10,448]{2,1,0:T(8,128)(2,1)}), bf16[16,10,448]{2,1,0:T(8,128)(2,1)S(1)}, u32[]{:S(2)}, u32[]{:S(2)}) async-start(bf16[16,10,448]{2,1,0:T(8,128)(2,1)} %copy.125), calls=%async_computation.1 | async-start | bytes 524288 | tf_op jit(solution)/shard_map/all_to_all | solution.py:77
  322.0 12.7 %all-to-all-start.3 = ((bf16[16,10,448]{2,1,0:T(8,128)(2,1)}), bf16[16,10,448]{2,1,0:T(8,128)(2,1)S(1)}, u32[]{:S(2)}, u32[]{:S(2)}) async-start(bf16[16,10,448]{2,1,0:T(8,128)(2,1)} %copy.137), calls=%async_computation.3 | async-start | bytes 524288 | tf_op jit(solution)/shard_map/all_to_all | solution.py:103
  327.7 37.0 %collective-permute-start.8 = (bf16[1,128,7168]{2,1,0:T(8,128)(2,1)S(1)}, bf16[1,128,7168]{2,1,0:T(8,128)(2,1)}, u32[]{:S(2)}, u32[]{:S(2)}) collective-permute-start(bf16[1,128,7168]{2,1,0:T(8,128)(2,1)S(1)} %fusion.1), channel_id=1, source_target_pairs={{0,16},{16,0},{1,17},{17,1},{2,18},{18,2},{3,19},{19,3},{4,20},{20... | collective-permute-start | bytes 5505032 | tf_op jit(solution)/shard_map/ppermute | solution.py:18
  337.8 26.9 %collective-permute-start.17 = (bf16[1,128,7168]{2,1,0:T(8,128)(2,1)}, bf16[1,128,7168]{2,1,0:T(8,128)(2,1)}, u32[]{:S(2)}, u32[]{:S(2)}) collective-permute-start(bf16[1,128,7168]{2,1,0:T(8,128)(2,1)} %fusion.2), channel_id=1, source_target_pairs={{0,16},{16,0},{1,17},{17,1},{2,18},{18,2},{3,19},{19,3},{4,20},{20... | collective-permute-start | bytes 5505032 | tf_op jit(solution)/shard_map/ppermute | solution.py:18
  337.9 4.6 %collective-permute-start.18 = (bf16[16,10]{1,0:T(8,128)(2,1)S(1)}, bf16[16,10]{1,0:T(8,128)(2,1)S(1)}, u32[]{:S(2)}, u32[]{:S(2)}) collective-permute-start(bf16[16,10]{1,0:T(8,128)(2,1)S(1)} %reshape.360), channel_id=1, source_target_pairs={{0,8},{1,9},{2,10},{3,11},{4,12},{5,13},{6,14},{7,15},{8,0},{9,1},... | collective-permute-start | bytes 968 | tf_op jit(solution)/shard_map/ppermute | solution.py:12
  342.5 3.6 collective-permute-start.19
  346.1 3.6 collective-permute-start.20
  349.7 3.6 collective-permute-start.21
  364.7 5.8 %copy-start.1 = (bf16[1,7168,128]{2,1,0:T(8,128)(2,1)S(1)}, bf16[1,7168,128]{2,1,0:T(8,128)(2,1)}, u32[]{:S(2)}) copy-start(bf16[1,7168,128]{2,1,0:T(8,128)(2,1)} %param.17) | copy-start | bytes 5505028
where the time goes:
time: 372 us; the launch traced here: 371 us
  waiting for transfers between devices  201 us (54%)
  local copies, waits for them, and re-layouts  60.6 us (16%)
  starting transfers between devices  43.3 us (12%)
  other arithmetic  30.4 us (8%)
  matrix products  23.2 us (6%)
  blocking collectives  10.6 us (3%)
    ppermute x20, waiting for transfers between devices, from_partner(): return lax.ppermute(value, axis, pairs)  172 us
    ppermute x20, starting transfers between devices, from_partner(): return lax.ppermute(value, axis, pairs)  23.8 us
    select_n x12, other arithmetic, send_rows(): jnp.where(upper_side, jnp.concatenate([partner, received], axis=2), jnp.c...  15.8 us
    all_to_all x2, waiting for transfers between devices, send_rows(): lax.all_to_all(pieces, 'expert', split_axis=0, concat_axis=0, tiled=True)  13.9 us
    concatenate x10, local copies, waits for them, and re-layouts, send_rows(): jnp.concatenate([partner, received], axis=2)  13.6 us
    all_to_all x2, starting transfers between devices, send_rows(): lax.all_to_all(pieces, 'expert', split_axis=0, concat_axis=0, tiled=True)  11.9 us
    all_to_all x1, blocking collectives, return_grads(): lax.all_to_all(dot_totals.astype(jnp.bfloat16), 'expert', split_axis=0, c...  10.6 us
    ppermute x4, local copies, waits for them, and re-layouts, from_partner(): return lax.ppermute(value, axis, pairs)  8.79 us
  transfers between devices with their start and end apart: 26, of which 19 were waited for; matrix products, arithmetic and copies ran while one was open for 27% of the time, Pallas kernels for 0%

commit v1 on v0

v1 whole, which is shorter than its diff:
```python
import functools
import math

import jax
import jax.numpy as jnp
from jax import lax
from jax.experimental import pallas as pl
from jax.experimental.pallas import tpu as pltpu
from jax.sharding import PartitionSpec as P

FF = 2048
QUAD = 4
MESH = pl.DeviceIdType.MESH


def from_behind(value, axis, steps):
    count = lax.axis_size(axis)
    pairs = [(source, (source + steps) % count) for source in range(count)]
    return lax.ppermute(value, axis, pairs)


def routing(ids, gates, experts, capacity):
    expert_ids = jnp.arange(experts, dtype=jnp.int32)
    matches = ids[None, :, :] == expert_ids[:, None, None]
    routed = jnp.any(matches, axis=2)
    weights = jnp.sum(jnp.where(matches, gates[None, :, :], 0.0), axis=2)
    tokens = ids.shape[0]
    earlier = jnp.arange(tokens)[:, None] <= jnp.arange(tokens)[None, :]
    counted = jnp.sum(jnp.where(routed[:, :, None] & earlier[None], 1, 0), axis=1)
    position = counted - 1
    slot_ids = jnp.arange(capacity, dtype=jnp.int32)
    placing = (position[:, None, :] == slot_ids[None, :, None]) & routed[:, None, :]
    return (matches, placing.astype(jnp.float32), weights)


def xor(value, mask):
    out = value
    bit = 1
    while bit <= mask:
        if mask & bit:
            out = out + bit - 2 * bit * ((value // bit) % 2)
        bit *= 2
    return out


def dot(a, b, dims=((1,), (0,)), precision=None):
    return lax.dot_general(
        a, b, (dims, ((), ())), preferred_element_type=jnp.float32, precision=precision
    )


class Links:
    def __init__(self, send_sems, recv_sems):
        self.send_sems = send_sems
        self.recv_sems = recv_sems
        self.count = 0
        self.sent = []

    def copy(self, src, dst, peer):
        k = self.count
        self.count += 1
        return pltpu.make_async_remote_copy(
            src_ref=src,
            dst_ref=dst,
            send_sem=self.send_sems.at[k],
            recv_sem=self.recv_sems.at[k],
            device_id={"expert": peer},
            device_id_type=MESH,
        )

    def start(self, copy):
        copy.start()
        self.sent.append(copy)


def layer_kernel(
    slices,
    chunks,
    tok_f,
    tok_b,
    w_gate,
    w_up,
    w_down,
    place_f,
    place_b,
    pre_gate,
    pre_up,
    rid_ref,
    fold_ref,
    unfold_ref,
    spread_ref,
    collect_ref,
    out_f,
    out_b,
    out_dots,
    tok,
    wc,
    wd,
    gat,
    par,
    rs1,
    rs2,
    rsz,
    hold,
    hold2,
    acc_ref,
    dot_ref,
    dot_got,
    local_sems,
    send_sems,
    recv_sems,
):
    device = lax.axis_index("expert")
    me = device % slices
    base = device - me
    lo = me % QUAD
    z = me // QUAD
    depth = slices // QUAD
    xp = base + xor(me, 1)
    yp = base + xor(me, 2)
    zp = [base + xor(z, q) * QUAD + lo for q in range(depth)]
    partners = [xp, yp] + zp[1:]
    width = wd.shape[2]
    ff = wd.shape[1]

    loads = []

    def load(src, dst):
        copy = pltpu.make_async_copy(src, dst, local_sems.at[len(loads)])
        loads.append(copy)
        copy.start()
        return copy

    load_tok = [load(tok_f, tok.at[0]), load(tok_b, tok.at[1])]
    load_w = []
    for j in range(chunks):
        rows = pl.ds(j * width, width)
        load_w.append(load(w_gate.at[rows, :], wc.at[j, :, pl.ds(0, ff)]))
        load_w.append(load(w_up.at[rows, :], wc.at[j, :, pl.ds(ff, ff)]))
        load_w.append(load(w_down.at[:, rows], wd.at[j]))

    barrier = pltpu.get_barrier_semaphore()
    for peer in partners:
        pl.semaphore_signal(barrier, inc=1, device_id={"expert": peer}, device_id_type=MESH)

    block_rows = gat.shape[2]
    group_rows = QUAD * block_rows
    places = (place_f, place_b)

    def place(mb):
        rid = rid_ref[:block_rows, :1]
        chosen = places[mb][...]
        total = jnp.zeros((block_rows, width), jnp.float32)
        for j in range(chunks):
            part = jnp.where(rid == j, chosen, 0.0).astype(jnp.bfloat16)
            total = total + dot(part, tok[mb, :, pl.ds(j * width, width)])
        gat[mb, me] = total.astype(jnp.bfloat16)

    links = Links(send_sems, recv_sems)

    def bid(q, mask):
        return xor(z, q) * QUAD + xor(lo, mask)

    steps = [(mb, q) for mb in range(2) for q in range(depth)]
    zsend = {}
    own_x, own_y, forward = {}, {}, {}
    r1, r2, rz = {}, {}, {}
    for mb, q in steps:
        if q > 0:
            zsend[mb, q] = links.copy(gat.at[mb, me], gat.at[mb, me], zp[q])
        block = gat.at[mb, bid(q, 0)]
        own_x[mb, q] = links.copy(block, block, xp)
        own_y[mb, q] = links.copy(block, block, yp)
        first = q % 2 == 0
        got = gat.at[mb, bid(q, 2 if first else 1)]
        forward[mb, q] = links.copy(got, got, xp if first else yp)
        m1, p1, m2, p2 = (1, xp, 2, yp) if first else (2, yp, 1, xp)
        r1[mb, q] = [
            links.copy(par.at[mb, bid(q, m1)], rs1.at[mb, q, 0], p1),
            links.copy(par.at[mb, bid(q, 3)], rs1.at[mb, q, 1], p1),
        ]
        r2[mb, q] = links.copy(hold.at[mb, q], rs2.at[mb, q], p2)
        if q > 0:
            rz[mb, q] = links.copy(hold2.at[mb, q], rsz.at[mb, q], zp[q])
    dx = links.copy(dot_ref.at[0], dot_got.at[0], xp)
    dy = links.copy(dot_ref.at[1], dot_got.at[1], yp)
    dz = [links.copy(dot_ref.at[2], dot_got.at[1 + q], zp[q]) for q in range(1, depth)]

    def own_sends(mb, q):
        if q > 0:
            zsend[mb, q].wait_recv()
        links.start(own_x[mb, q])
        links.start(own_y[mb, q])

    def start_mb(mb):
        for q in range(1, depth):
            links.start(zsend[mb, q])

    def do_forward(mb, q):
        (own_y if q % 2 == 0 else own_x)[mb, q].wait_recv()
        links.start(forward[mb, q])

    def compute(mb, q):
        (own_x if q % 2 == 0 else own_y)[mb, q].wait_recv()
        forward[mb, q].wait_recv()
        zq = xor(z, q)
        rid = rid_ref[...]
        group = pl.ds(zq * QUAD, QUAD)
        buf = gat[mb, group].reshape(group_rows, width)
        half = rid[:, :ff]
        fold = fold_ref[...]
        unfold = unfold_ref[...]
        if mb == 0:

            def gather_step(j, acc):
                return jnp.where(rid == j.astype(jnp.float32), dot(buf, wc[j]), acc)

            acc = lax.fori_loop(0, chunks, gather_step, jnp.zeros((group_rows, 2 * ff), jnp.float32))
            act = dot(fold, acc, precision=lax.Precision.HIGHEST)
            gate = act[:, :ff]
            hidden = gate / (1.0 + jnp.exp(-gate)) * act[:, ff:]
            spread = dot(unfold, hidden.astype(jnp.bfloat16))
            acc_ref[...] = jnp.zeros_like(acc_ref)

            def out_step(j, carry):
                part = jnp.where(half == j.astype(jnp.float32), spread, 0.0).astype(jnp.bfloat16)
                acc_ref[...] += dot(part, wd[j])
                return carry

            lax.fori_loop(0, chunks, out_step, 0)
        else:

            def gather_step(j, acc):
                return jnp.where(
                    half == j.astype(jnp.float32), dot(buf, wd[j], ((1,), (1,))), acc
                )

            acc = lax.fori_loop(0, chunks, gather_step, jnp.zeros((group_rows, ff), jnp.float32))
            grad = dot(fold, acc, precision=lax.Precision.HIGHEST)
            count = grad.shape[0]
            gate = pre_gate[zq].astype(jnp.float32)
            up = pre_up[zq].astype(jnp.float32)
            sig = 1.0 / (1.0 + jnp.exp(-gate))
            activated = gate * sig
            dots = jnp.sum(grad * activated * up, axis=1, keepdims=True)
            tile = dot(
                collect_ref[...], dots * spread_ref[...], precision=lax.Precision.HIGHEST
            )
            dot_ref[0, zq] = tile
            grad_gate = (grad * up * sig * (1.0 + gate * (1.0 - sig))).astype(jnp.bfloat16)
            grad_up = (grad * activated).astype(jnp.bfloat16)
            spread = jnp.concatenate([dot(unfold, grad_gate), dot(unfold, grad_up)], axis=1)
            acc_ref[...] = jnp.zeros_like(acc_ref)

            def out_step(j, carry):
                part = jnp.where(rid == j.astype(jnp.float32), spread, 0.0).astype(jnp.bfloat16)
                acc_ref[...] += dot(part, wc[j], ((1,), (1,)))
                return carry

            lax.fori_loop(0, chunks, out_step, 0)
        par[mb, group] = acc_ref[...].astype(jnp.bfloat16).reshape(QUAD, block_rows, width)
        for copy in r1[mb, q]:
            links.start(copy)

    def wide(value):
        return value.astype(jnp.float32)

    def second(mb, q):
        for copy in r1[mb, q]:
            copy.wait_recv()
        m2 = 2 if q % 2 == 0 else 1
        total = wide(par[mb, bid(q, m2)]) + wide(rs1[mb, q, 1])
        hold[mb, q] = total.astype(jnp.bfloat16)
        links.start(r2[mb, q])

    def third(mb, q):
        r2[mb, q].wait_recv()
        total = wide(par[mb, bid(q, 0)]) + wide(rs1[mb, q, 0]) + wide(rs2[mb, q])
        hold2[mb, q] = total.astype(jnp.bfloat16)
        if q > 0:
            links.start(rz[mb, q])

    def finish(mb, out):
        total = wide(hold2[mb, 0])
        for q in range(1, depth):
            rz[mb, q].wait_recv()
            total = total + wide(rsz[mb, q])
        out[...] = total.astype(jnp.bfloat16)

    load_tok[0].wait()
    place(0)
    pl.semaphore_wait(barrier, len(partners))
    start_mb(0)
    own_sends(*steps[0])
    load_tok[1].wait()
    place(1)
    for copy in load_w:
        copy.wait()
    count = len(steps)
    for t in range(count + 3):
        if t + 1 < count:
            if t + 1 == 2:
                start_mb(1)
            own_sends(*steps[t + 1])
        if t < count:
            do_forward(*steps[t])
        if 0 <= t - 1 < count:
            compute(*steps[t - 1])
        if t - 1 == count - 1:
            links.start(dx)
        if 0 <= t - 2 < count:
            second(*steps[t - 2])
        if t - 2 == count - 1:
            dx.wait_recv()
            dot_ref[1] = dot_ref[0] + dot_got[0]
            links.start(dy)
        if 0 <= t - 3 < count:
            third(*steps[t - 3])
    finish(0, out_f)
    dy.wait_recv()
    dot_ref[2] = dot_ref[1] + dot_got[1]
    for copy in dz:
        links.start(copy)
    finish(1, out_b)
    total = dot_ref[2]
    for q in range(1, depth):
        dz[q - 1].wait_recv()
        total = total + dot_got[1 + q]
    out_dots[...] = total
    for copy in links.sent:
        copy.wait_send()


def run_layer(tok_f, tok_b, w_gate, w_up, w_down, place_f, place_b, pre_gate, pre_up, slices, rows):
    features = tok_f.shape[1]
    chunks = 16 // math.gcd(16, rows)
    width = features // chunks
    ff = w_gate.shape[1]
    depth = slices // QUAD
    block_rows = chunks * rows
    group_rows = QUAD * block_rows
    group_slots = QUAD * rows

    row = jnp.arange(group_rows)
    slot = (row // block_rows) * rows + row % rows
    rid = jnp.broadcast_to((row % block_rows // rows)[:, None], (group_rows, 2 * ff))
    rid = rid.astype(jnp.float32)
    unfold = (slot[:, None] == jnp.arange(group_slots)[None, :])
    fold = unfold.T.astype(jnp.float32)
    unfold = unfold.astype(jnp.bfloat16)
    slots = jnp.arange(group_slots)
    spread = (slots[:, None] % rows == jnp.arange(128)[None, :]).astype(jnp.float32)
    collect = (slots[None, :] // rows == jnp.arange(8)[:, None]).astype(jnp.float32)

    vmem = pl.BlockSpec(memory_space=pltpu.VMEM)
    anywhere = pl.BlockSpec(memory_space=pl.ANY)
    block = (block_rows, width)
    sems = 2 * (depth * 6 + 2 * (depth - 1)) + 2 + depth - 1
    return pl.pallas_call(
        functools.partial(layer_kernel, slices, chunks),
        out_shape=(
            jax.ShapeDtypeStruct(block, jnp.bfloat16),
            jax.ShapeDtypeStruct(block, jnp.bfloat16),
            jax.ShapeDtypeStruct((depth, 8, 128), jnp.float32),
        ),
        in_specs=[anywhere] * 5 + [vmem] * 9,
        out_specs=(vmem, vmem, vmem),
        scratch_shapes=[
            pltpu.VMEM((2,) + tok_f.shape, jnp.bfloat16),
            pltpu.VMEM((chunks, width, 2 * ff), jnp.bfloat16),
            pltpu.VMEM((chunks, ff, width), jnp.bfloat16),
            pltpu.VMEM((2, slices) + block, jnp.bfloat16),
            pltpu.VMEM((2, slices) + block, jnp.bfloat16),
            pltpu.VMEM((2, depth, 2) + block, jnp.bfloat16),
            pltpu.VMEM((2, depth) + block, jnp.bfloat16),
            pltpu.VMEM((2, depth) + block, jnp.bfloat16),
            pltpu.VMEM((2, depth) + block, jnp.bfloat16),
            pltpu.VMEM((2, depth) + block, jnp.bfloat16),
            pltpu.VMEM((group_rows, width), jnp.float32),
            pltpu.VMEM((3, depth, 8, 128), jnp.float32),
            pltpu.VMEM((1 + depth, depth, 8, 128), jnp.float32),
            pltpu.SemaphoreType.DMA((2 + 3 * chunks,)),
            pltpu.SemaphoreType.DMA((sems,)),
            pltpu.SemaphoreType.DMA((sems,)),
        ],
        compiler_params=pltpu.CompilerParams(
            collective_id=0, has_side_effects=True, vmem_limit_bytes=56 * 2**20
        ),
        name="moe_layer",
    )(tok_f, tok_b, w_gate, w_up, w_down, place_f, place_b, pre_gate, pre_up,
      rid, fold, unfold, spread, collect)


def mix_kernel(rows, block_f, block_b, weight_f, weight_b, out_f, out_b):
    block_rows, width = block_f.shape
    j = pl.program_id(0)
    low = j * rows
    column = lax.broadcasted_iota(jnp.int32, weight_f.shape, 1)
    inside = (column >= low) & (column < low + rows)
    for block, weight, out in ((block_f, weight_f, out_f), (block_b, weight_b, out_b)):
        wanted = jnp.where(inside, weight[...], 0.0)
        high = wanted.astype(jnp.bfloat16)
        rest = (wanted - high.astype(jnp.float32)).astype(jnp.bfloat16)
        out[...] = (dot(high, block[...]) + dot(rest, block[...])).astype(jnp.bfloat16)


def mix(block_f, block_b, weight_f, weight_b, rows):
    block_rows, width = block_f.shape
    tokens = weight_f.shape[0]
    chunks = block_rows // rows
    whole = pl.BlockSpec(block_f.shape, lambda j: (0, 0))
    weights = pl.BlockSpec(weight_f.shape, lambda j: (0, 0))
    piece = pl.BlockSpec((tokens, width), lambda j: (0, j))
    shape = jax.ShapeDtypeStruct((tokens, chunks * width), jnp.bfloat16)
    return pl.pallas_call(
        functools.partial(mix_kernel, rows),
        out_shape=(shape, shape),
        grid=(chunks,),
        in_specs=[whole, whole, weights, weights],
        out_specs=(piece, piece),
        name="mix",
    )(block_f, block_b, weight_f, weight_b)


def body(
    act_in,
    cotangent,
    fwd_ids,
    fwd_gates,
    bwd_ids,
    bwd_gates,
    gate_w,
    up_w,
    down_w,
    gate_pre,
    up_pre,
):
    ndev = lax.axis_size("expert")
    ff_dev = gate_w.shape[2]
    slices = FF // ff_dev
    experts = ndev // slices
    capacity = gate_pre.shape[1] // ndev
    rows = experts * capacity
    chunks = 16 // math.gcd(16, rows)
    features = act_in.shape[2]
    width = features // chunks
    depth = slices // QUAD
    columns = [[g * slices + i for g in range(experts)] for i in range(slices)]

    def exchange(value):
        return lax.all_to_all(
            value, "expert", split_axis=0, concat_axis=0, axis_index_groups=columns, tiled=True
        )

    matches_f, placing_f, weights_f = routing(fwd_ids[0], fwd_gates[0], experts, capacity)
    matches_b, placing_b, weights_b = routing(bwd_ids[0], bwd_gates[0], experts, capacity)

    def prepare(tokens, placing):
        chosen = placing.reshape(rows, tokens.shape[0])
        if experts > 1:
            picked = dot(chosen.astype(jnp.bfloat16), tokens).astype(jnp.bfloat16)
            picked = exchange(picked.reshape(experts, capacity, features))
            tokens = picked.reshape(rows, features)
            chosen = jnp.eye(rows, dtype=jnp.float32)
        return tokens, jnp.tile(chosen, (chunks, 1))

    tok_f, place_f = prepare(act_in[0], placing_f)
    tok_b, place_b = prepare(cotangent[0], placing_b)

    def by_group(saved):
        saved = saved.reshape(experts, slices, capacity, ff_dev).transpose(1, 0, 2, 3)
        return saved.reshape(depth, QUAD * rows, ff_dev)

    block_f, block_b, dots = run_layer(
        tok_f, tok_b, gate_w[0], up_w[0], down_w[0], place_f, place_b,
        by_group(gate_pre[0]), by_group(up_pre[0]), slices, rows,
    )
    me = lax.axis_index("expert") % slices
    mine = lax.dynamic_slice(dots, (me // QUAD, me % QUAD, 0), (1, 1, 128))
    mine = mine[0, 0, :rows].reshape(experts, capacity)

    def send_back(block):
        table = block.reshape(chunks, rows, width).transpose(1, 0, 2)
        table = exchange(table.reshape(experts, capacity, features))
        table = table.reshape(rows, chunks, width).transpose(1, 0, 2)
        return table.reshape(chunks * rows, width)

    if experts > 1:
        block_f = send_back(block_f)
        block_b = send_back(block_b)
        mine = exchange(mine)

    token_dots = jnp.sum(placing_b * mine[:, :, None], axis=1)
    gate_grad = jnp.sum(jnp.where(matches_b, token_dots[:, :, None], 0.0), axis=0)

    def weight_table(placing, weights):
        table = (placing * weights[:, None, :]).reshape(rows, -1).T
        return jnp.tile(table, (1, chunks))

    weight_f = from_behind(weight_table(placing_f, weights_f), "section", 1)
    weight_b = from_behind(weight_table(placing_b, weights_b), "section", -1)
    block_f = from_behind(block_f, "section", 1)
    block_b = from_behind(block_b, "section", -1)
    next_act, prev_grad = mix(block_f, block_b, weight_f, weight_b, rows)
    return (next_act[None], prev_grad[None], gate_grad[None])


def solution(mesh):
    in_specs = (
        P("section", "expert", None),
        P("section", "expert", None),
        P("section", "expert", None),
        P("section", "expert", None),
        P("section", "expert", None),
        P("section", "expert", None),
        P("section", None, "expert"),
        P("section", None, "expert"),
        P("section", "expert", None),
        P("section", None, "expert"),
        P("section", None, "expert"),
    )
    out_specs = (
        P("section", "expert", None),
        P("section", "expert", None),
        P("section", "expert", None),
    )
    return jax.shard_map(body, mesh=mesh, in_specs=in_specs, out_specs=out_specs, check_vma=False)
```

time: 372 us -> 128 us (0.34)
  waiting for transfers between devices: 201 us -> 0.01 us
  Pallas kernels: 0 us -> 117 us
  local copies, waits for them, and re-layouts: 60.6 us -> 4.29 us
  starting transfers between devices: 43.3 us -> 1.21 us
  other arithmetic: 30.4 us -> 5.13 us
  matrix products: 23.2 us -> 0 us
  blocking collectives: 10.6 us -> 0 us
    ppermute x20 -> x0, waiting for transfers between devices: 172 us -> none  [from_partner(): return lax.ppermute(value, axis, pairs)]
    pallas_call x0 -> x2, Pallas kernels: none -> 117 us  [the longest x1 111 us: run_layer(): pl.pallas_call(functools.partial(layer_kernel, slices, chunks), out_shape...]
    all_to_all x4 -> x0, waiting for transfers between devices: 28.9 us -> none  [the longest x2 13.9 us: send_rows(): lax.all_to_all(pieces, 'expert', split_axis=0, concat_axis=0, tiled=True)]
    ppermute x20 -> x0, starting transfers between devices: 23.8 us -> none  [from_partner(): return lax.ppermute(value, axis, pairs)]
    dot_general x10 -> x0, matrix products: 23.2 us -> none  [the longest x1 5.16 us: body(): jnp.dot(hidden, w_down, preferred_element_type=jnp.float32)]
    all_to_all x4 -> x0, starting transfers between devices: 19.4 us -> none  [the longest x2 11.9 us: send_rows(): lax.all_to_all(pieces, 'expert', split_axis=0, concat_axis=0, tiled=True)]
    select_n x12 -> x2, other arithmetic: 15.8 us -> 0.02 us  [the longest x1 0.01 us: run_layer(): slots[None, :] // rows == jnp.arange(8)[:, None]]
    concatenate x10 -> x0, local copies, waits for them, and re-layouts: 13.6 us -> none  [send_rows(): jnp.concatenate([partner, received], axis=2)]
  transfers between devices with their start and end apart: 26 -> 4, of which waited for: 19 -> 0; matrix products, arithmetic and copies ran while one was open for 27% -> 6% of each run, Pallas kernels for 0% -> 87%
where the time goes in v1:
time: 128 us
  Pallas kernels  117 us (91%)
  other arithmetic  5.13 us (4%)
  local copies, waits for them, and re-layouts  4.29 us (3%)
    pallas_call x1, Pallas kernels, run_layer(): pl.pallas_call(functools.partial(layer_kernel, slices, chunks), out_shape...  111 us
    pallas_call x1, Pallas kernels, mix(): pl.pallas_call(functools.partial(mix_kernel, rows), out_shape=(shape, sha...  5.71 us
  transfers between devices with their start and end apart: 4, of which 0 were waited for; matrix products, arithmetic and copies ran while one was open for 6% of the time, Pallas kernels for 87%

profile of v1, /device:TPU:0, one launch (start us, length us, event | category | flops | bytes accessed | tf_op | source)
XLA Modules:
  0.0 128.0 jit_solution(5899320760074716961)
XLA Ops:
  0.6 0.7 select_reduce_fusion.2
  1.4 0.1 select_reduce_fusion
  1.5 0.1 copy.17
  1.6 0.6 collective-permute-start.3
  2.2 0.7 select_reduce_fusion.3
  2.9 0.1 select_reduce_fusion.1
  3.1 0.1 copy.16
  3.2 0.1 collective-permute-start.2
  3.3 0.6 fusion.3.fold_ref
  4.0 0.7 fusion.unfold_ref
  4.7 0.6 fusion.18.collect_ref
  5.3 0.7 fusion.4.spread_ref
  6.0 0.6 tile.37.place_b
  6.6 0.6 tile.17.place_f
  7.3 0.8 broadcast_in_dim.29.rid_ref
  8.1 110.9 %moe_layer.1 = (bf16[80,896]{1,0:T(8,128)(2,1)}, bf16[80,896]{1,0:T(8,128)(2,1)}, f32[4,8,128]{2,1,0:T(8,128)}) custom-call(bf16[128,7168]{1,0:T(8,128)(2,1)} %bitcast.15, bf16[128,7168]{1,0:T(8,128)(2,1)} %bitcast.16, bf16[7168,128]{1,0:T(8,128)(2,1)} %bitcast.17, bf16[7168,128]{1,0:T(8,128)(2,1)} %bitcast.18, bf16[128,7168]{1,0:T(8,128)(2,1)} %bitcast.19, ...), custom_call_target="tpu_custom_call" | custom-call | tf_op jit(solution)/shard_map/moe_layer/pallas_call | solution.py:359
  119.0 0.1 collective-permute-start
  119.1 0.5 collective-permute-start.1
  119.6 0.7 constant_dynamic-slice_fusion
  120.3 0.1 fusion.13
  120.3 0.6 broadcast_select_fusion
  121.0 0.0 collective-permute-done.3.weight_b
  121.0 0.0 copy-start.2
  121.0 0.0 collective-permute-done.2.weight_f
  121.0 0.0 copy-start.3
  121.0 0.0 collective-permute-done.block_f
  121.0 0.0 copy-start
  121.0 0.0 collective-permute-done.1.block_b
  121.0 0.6 copy-done.2
  121.6 0.0 copy-done.3
  121.6 0.1 copy-done
  121.7 0.0 copy-start.1
  121.7 0.6 copy-done.1
  122.3 5.7 %mix.1 = (bf16[128,7168]{1,0:T(8,128)(2,1)}, bf16[128,7168]{1,0:T(8,128)(2,1)}) custom-call(bf16[80,896]{1,0:T(8,128)(2,1)} %copy-done, bf16[80,896]{1,0:T(8,128)(2,1)} %copy-done.1, f32[128,80]{1,0:T(8,128)} %copy-done.3, f32[128,80]{1,0:T(8,128)} %copy-done.2), custom_call_target="tpu_custom_call" | custom-call | tf_op jit(solution)/shard_map/mix/pallas_call | solution.py:415
  (19 shorter events, 0.2 us)
Async XLA Ops:
  1.6 119.3 %collective-permute-start.3 = (f32[128,80]{1,0:T(8,128)S(1)}, f32[128,80]{1,0:T(8,128)S(1)}, u32[]{:S(2)}, u32[]{:S(2)}) collective-permute-start(f32[128,80]{1,0:T(8,128)S(1)} %copy.17), channel_id=1, source_target_pairs={{0,16},{16,0},{1,17},{17,1},{2,18},{18,2},{3,19},{19,3},{4,20},{20... | collective-permute-start | bytes 122888 | tf_op jit(solution)/shard_map/ppermute | solution.py:19
  3.2 117.8 %collective-permute-start.2 = (f32[128,80]{1,0:T(8,128)S(1)}, f32[128,80]{1,0:T(8,128)S(1)}, u32[]{:S(2)}, u32[]{:S(2)}) collective-permute-start(f32[128,80]{1,0:T(8,128)S(1)} %copy.16), channel_id=1, source_target_pairs={{0,16},{16,0},{1,17},{17,1},{2,18},{18,2},{3,19},{19,3},{4,20},{20... | collective-permute-start | bytes 122888 | tf_op jit(solution)/shard_map/ppermute | solution.py:19
  119.0 2.0 %collective-permute-start = (bf16[80,896]{1,0:T(8,128)(2,1)}, bf16[80,896]{1,0:T(8,128)(2,1)S(1)}, u32[]{:S(2)}, u32[]{:S(2)}) collective-permute-start(bf16[80,896]{1,0:T(8,128)(2,1)} %get-tuple-element.8), channel_id=1, source_target_pairs={{0,16},{16,0},{1,17},{17,1},{2,18},{18,2},{3,19},{19,3},{4,20},{20... | collective-permute-start | bytes 430088 | tf_op jit(solution)/shard_map/ppermute | solution.py:19
  119.1 1.9 %collective-permute-start.1 = (bf16[80,896]{1,0:T(8,128)(2,1)}, bf16[80,896]{1,0:T(8,128)(2,1)S(1)}, u32[]{:S(2)}, u32[]{:S(2)}) collective-permute-start(bf16[80,896]{1,0:T(8,128)(2,1)} %get-tuple-element.9), channel_id=1, source_target_pairs={{0,16},{16,0},{1,17},{17,1},{2,18},{18,2},{3,19},{19,3},{4,20},{20... | collective-permute-start | bytes 430088 | tf_op jit(solution)/shard_map/ppermute | solution.py:19
  121.0 0.6 copy-start.2
  121.0 0.7 copy-start.3
  121.0 0.7 copy-start
  121.7 0.6 copy-start.1

commit v2 on v1

--- a/solution.py
+++ b/solution.py
@@ -3,6 +3,7 @@
 
 import jax
 import jax.numpy as jnp
+import numpy as np
 from jax import lax
 from jax.experimental import pallas as pl
 from jax.experimental.pallas import tpu as pltpu
@@ -56,7 +57,7 @@
         self.count = 0
         self.sent = []
 
-    def copy(self, src, dst, peer):
+    def copy(self, src, dst, peer, axis="expert"):
         k = self.count
         self.count += 1
         return pltpu.make_async_remote_copy(
@@ -64,7 +65,7 @@
             dst_ref=dst,
             send_sem=self.send_sems.at[k],
             recv_sem=self.recv_sems.at[k],
-            device_id={"expert": peer},
+            device_id={axis: peer},
             device_id_type=MESH,
         )
 
@@ -76,6 +77,7 @@
 def layer_kernel(
     slices,
     chunks,
+    hop,
     tok_f,
     tok_b,
     w_gate,
@@ -103,6 +105,8 @@
     rsz,
     hold,
     hold2,
+    sums,
+    landed,
     acc_ref,
     dot_ref,
     dot_got,
@@ -131,17 +135,20 @@
         copy.start()
         return copy
 
-    load_tok = [load(tok_f, tok.at[0]), load(tok_b, tok.at[1])]
-    load_w = []
-    for j in range(chunks):
-        rows = pl.ds(j * width, width)
-        load_w.append(load(w_gate.at[rows, :], wc.at[j, :, pl.ds(0, ff)]))
-        load_w.append(load(w_up.at[rows, :], wc.at[j, :, pl.ds(ff, ff)]))
-        load_w.append(load(w_down.at[:, rows], wd.at[j]))
+    load_tok = [load(tok_f, tok.at[0])]
 
     barrier = pltpu.get_barrier_semaphore()
     for peer in partners:
         pl.semaphore_signal(barrier, inc=1, device_id={"expert": peer}, device_id_type=MESH)
+    greeted = len(partners)
+    if hop:
+        section = lax.axis_index("section")
+        sections = lax.axis_size("section")
+        ahead = (section + 1) % sections
+        behind = (section + sections - 1) % sections
+        for peer in (ahead, behind):
+            pl.semaphore_signal(barrier, inc=1, device_id={"section": peer}, device_id_type=MESH)
+        greeted += 2
 
     block_rows = gat.shape[2]
     group_rows = QUAD * block_rows
@@ -161,48 +168,65 @@
     def bid(q, mask):
         return xor(z, q) * QUAD + xor(lo, mask)
 
-    steps = [(mb, q) for mb in range(2) for q in range(depth)]
-    zsend = {}
+    order = list(range(1, depth)) + [0]
+    steps = [(0, q) for q in range(depth)] + [(1, q) for q in order]
+    tiles = width // 128
+    cut = tiles // 2 * 128
+    zsend, parts = {}, {}
     own_x, own_y, forward = {}, {}, {}
     r1, r2, rz = {}, {}, {}
-    for mb, q in steps:
+    for step in steps:
+        mb, q = step
+        if step == steps[-1]:
+            parts[step] = [(True, pl.ds(0, cut)), (False, pl.ds(cut, width - cut))]
+        else:
+            parts[step] = [(q % 2 == 0, pl.ds(0, width))]
         if q > 0:
-            zsend[mb, q] = links.copy(gat.at[mb, me], gat.at[mb, me], zp[q])
-        block = gat.at[mb, bid(q, 0)]
-        own_x[mb, q] = links.copy(block, block, xp)
-        own_y[mb, q] = links.copy(block, block, yp)
-        first = q % 2 == 0
-        got = gat.at[mb, bid(q, 2 if first else 1)]
-        forward[mb, q] = links.copy(got, got, xp if first else yp)
-        m1, p1, m2, p2 = (1, xp, 2, yp) if first else (2, yp, 1, xp)
-        r1[mb, q] = [
-            links.copy(par.at[mb, bid(q, m1)], rs1.at[mb, q, 0], p1),
-            links.copy(par.at[mb, bid(q, 3)], rs1.at[mb, q, 1], p1),
+            zsend[step] = links.copy(gat.at[mb, me], gat.at[mb, me], zp[q])
+            rz[step] = links.copy(hold2.at[mb, q], rsz.at[mb, q], zp[q])
+        own_x[step], own_y[step], forward[step], r1[step], r2[step] = [], [], [], [], []
+        for first, cols in parts[step]:
+            block = gat.at[mb, bid(q, 0), :, cols]
+            own_x[step].append(links.copy(block, block, xp))
+            own_y[step].append(links.copy(block, block, yp))
+            got = gat.at[mb, bid(q, 2 if first else 1), :, cols]
+            forward[step].append(links.copy(got, got, xp if first else yp))
+            m1, p1, p2 = (1, xp, yp) if first else (2, yp, xp)
+            r1[step].append([
+                links.copy(par.at[mb, bid(q, 3), :, cols], rs1.at[mb, q, 1, :, cols], p1),
+                links.copy(par.at[mb, bid(q, m1), :, cols], rs1.at[mb, q, 0, :, cols], p1),
+            ])
+            r2[step].append(links.copy(hold.at[mb, q, :, cols], rs2.at[mb, q, :, cols], p2))
+    if hop:
+        across = [
+            links.copy(sums.at[0], landed.at[0], ahead, "section"),
+            links.copy(sums.at[1], landed.at[1], behind, "section"),
         ]
-        r2[mb, q] = links.copy(hold.at[mb, q], rs2.at[mb, q], p2)
-        if q > 0:
-            rz[mb, q] = links.copy(hold2.at[mb, q], rsz.at[mb, q], zp[q])
     dx = links.copy(dot_ref.at[0], dot_got.at[0], xp)
     dy = links.copy(dot_ref.at[1], dot_got.at[1], yp)
     dz = [links.copy(dot_ref.at[2], dot_got.at[1 + q], zp[q]) for q in range(1, depth)]
 
-    def own_sends(mb, q):
-        if q > 0:
-            zsend[mb, q].wait_recv()
-        links.start(own_x[mb, q])
-        links.start(own_y[mb, q])
+    def own_sends(step):
+        if step[1] > 0:
+            zsend[step].wait_recv()
+        for copy_x, copy_y in zip(own_x[step], own_y[step]):
+            links.start(copy_x)
+            links.start(copy_y)
 
     def start_mb(mb):
         for q in range(1, depth):
             links.start(zsend[mb, q])
 
-    def do_forward(mb, q):
-        (own_y if q % 2 == 0 else own_x)[mb, q].wait_recv()
-        links.start(forward[mb, q])
-
-    def compute(mb, q):
-        (own_x if q % 2 == 0 else own_y)[mb, q].wait_recv()
-        forward[mb, q].wait_recv()
+    def do_forward(step):
+        for k, (first, cols) in enumerate(parts[step]):
+            (own_y if first else own_x)[step][k].wait_recv()
+            links.start(forward[step][k])
+
+    def compute(step):
+        mb, q = step
+        for k, (first, cols) in enumerate(parts[step]):
+            (own_x if first else own_y)[step][k].wait_recv()
+            forward[step][k].wait_recv()
         zq = xor(z, q)
         rid = rid_ref[...]
         group = pl.ds(zq * QUAD, QUAD)
@@ -220,14 +244,11 @@
             gate = act[:, :ff]
             hidden = gate / (1.0 + jnp.exp(-gate)) * act[:, ff:]
             spread = dot(unfold, hidden.astype(jnp.bfloat16))
-            acc_ref[...] = jnp.zeros_like(acc_ref)
-
-            def out_step(j, carry):
+
+            def piece(j, cols):
                 part = jnp.where(half == j.astype(jnp.float32), spread, 0.0).astype(jnp.bfloat16)
-                acc_ref[...] += dot(part, wd[j])
-                return carry
-
-            lax.fori_loop(0, chunks, out_step, 0)
+                return dot(part, wd[j, :, cols])
+
         else:
 
             def gather_step(j, acc):
@@ -250,88 +271,119 @@
             grad_gate = (grad * up * sig * (1.0 + gate * (1.0 - sig))).astype(jnp.bfloat16)
             grad_up = (grad * activated).astype(jnp.bfloat16)
             spread = jnp.concatenate([dot(unfold, grad_gate), dot(unfold, grad_up)], axis=1)
-            acc_ref[...] = jnp.zeros_like(acc_ref)
+
+            def piece(j, cols):
+                part = jnp.where(rid == j.astype(jnp.float32), spread, 0.0).astype(jnp.bfloat16)
+                return dot(part, wc[j, cols, :], ((1,), (1,)))
+
+        for k, (first, cols) in enumerate(parts[step]):
+            acc_ref[:, cols] = piece(jnp.int32(0), cols)
 
             def out_step(j, carry):
-                part = jnp.where(rid == j.astype(jnp.float32), spread, 0.0).astype(jnp.bfloat16)
-                acc_ref[...] += dot(part, wc[j], ((1,), (1,)))
+                acc_ref[:, cols] += piece(j, cols)
                 return carry
 
-            lax.fori_loop(0, chunks, out_step, 0)
-        par[mb, group] = acc_ref[...].astype(jnp.bfloat16).reshape(QUAD, block_rows, width)
-        for copy in r1[mb, q]:
-            links.start(copy)
+            lax.fori_loop(1, chunks, out_step, 0)
+            done = acc_ref[:, cols].astype(jnp.bfloat16)
+            par[mb, group, :, cols] = done.reshape(QUAD, block_rows, cols.size)
+            for copy in r1[step][k]:
+                links.start(copy)
 
     def wide(value):
         return value.astype(jnp.float32)
 
-    def second(mb, q):
-        for copy in r1[mb, q]:
-            copy.wait_recv()
-        m2 = 2 if q % 2 == 0 else 1
-        total = wide(par[mb, bid(q, m2)]) + wide(rs1[mb, q, 1])
-        hold[mb, q] = total.astype(jnp.bfloat16)
-        links.start(r2[mb, q])
-
-    def third(mb, q):
-        r2[mb, q].wait_recv()
-        total = wide(par[mb, bid(q, 0)]) + wide(rs1[mb, q, 0]) + wide(rs2[mb, q])
-        hold2[mb, q] = total.astype(jnp.bfloat16)
+    def second(step):
+        mb, q = step
+        for k, (first, cols) in enumerate(parts[step]):
+            r1[step][k][0].wait_recv()
+            m2 = 2 if first else 1
+            total = wide(par[mb, bid(q, m2), :, cols]) + wide(rs1[mb, q, 1, :, cols])
+            hold[mb, q, :, cols] = total.astype(jnp.bfloat16)
+            links.start(r2[step][k])
+
+    def third(step):
+        mb, q = step
+        for k, (first, cols) in enumerate(parts[step]):
+            r1[step][k][1].wait_recv()
+            r2[step][k].wait_recv()
+            total = wide(par[mb, bid(q, 0), :, cols]) + wide(rs1[mb, q, 0, :, cols])
+            total = total + wide(rs2[mb, q, :, cols])
+            hold2[mb, q, :, cols] = total.astype(jnp.bfloat16)
         if q > 0:
-            links.start(rz[mb, q])
-
-    def finish(mb, out):
+            links.start(rz[step])
+
+    def finish(mb):
         total = wide(hold2[mb, 0])
         for q in range(1, depth):
             rz[mb, q].wait_recv()
             total = total + wide(rsz[mb, q])
-        out[...] = total.astype(jnp.bfloat16)
+        sums[mb] = total.astype(jnp.bfloat16)
+        if hop:
+            links.start(across[mb])
+
+    def deliver(mb, out):
+        if hop:
+            across[mb].wait_recv()
+            out[...] = landed[mb]
+        else:
+            out[...] = sums[mb]
 
     load_tok[0].wait()
+    load_tok.append(load(tok_b, tok.at[1]))
+    load_w = []
+    for j in range(chunks):
+        rows = pl.ds(j * width, width)
+        load_w.append(load(w_gate.at[rows, :], wc.at[j, :, pl.ds(0, ff)]))
+        load_w.append(load(w_up.at[rows, :], wc.at[j, :, pl.ds(ff, ff)]))
+        load_w.append(load(w_down.at[:, rows], wd.at[j]))
     place(0)
-    pl.semaphore_wait(barrier, len(partners))
+    pl.semaphore_wait(barrier, greeted)
+    own_sends(steps[0])
     start_mb(0)
-    own_sends(*steps[0])
     load_tok[1].wait()
     place(1)
-    for copy in load_w:
-        copy.wait()
+    start_mb(1)
     count = len(steps)
     for t in range(count + 3):
         if t + 1 < count:
-            if t + 1 == 2:
-                start_mb(1)
-            own_sends(*steps[t + 1])
+            own_sends(steps[t + 1])
         if t < count:
-            do_forward(*steps[t])
+            do_forward(steps[t])
+        if t == 0:
+            for copy in load_w:
+                copy.wait()
         if 0 <= t - 1 < count:
-            compute(*steps[t - 1])
+            compute(steps[t - 1])
         if t - 1 == count - 1:
             links.start(dx)
         if 0 <= t - 2 < count:
-            second(*steps[t - 2])
+            second(steps[t - 2])
         if t - 2 == count - 1:
             dx.wait_recv()
             dot_ref[1] = dot_ref[0] + dot_got[0]
             links.start(dy)
         if 0 <= t - 3 < count:
-            third(*steps[t - 3])
-    finish(0, out_f)
+            third(steps[t - 3])
+        if t == count:
+            finish(0)
+        if t == count + 1:
+            deliver(0, out_f)
     dy.wait_recv()
     dot_ref[2] = dot_ref[1] + dot_got[1]
     for copy in dz:
         links.start(copy)
-    finish(1, out_b)
+    finish(1)
     total = dot_ref[2]
     for q in range(1, depth):
         dz[q - 1].wait_recv()
         total = total + dot_got[1 + q]
     out_dots[...] = total
+    deliver(1, out_b)
     for copy in links.sent:
         copy.wait_send()
 
 
-def run_layer(tok_f, tok_b, w_gate, w_up, w_down, place_f, place_b, pre_gate, pre_up, slices, rows):
+def run_layer(tok_f, tok_b, w_gate, w_up, w_down, place_f, place_b, pre_gate, pre_up, slices, rows, hop):
     features = tok_f.shape[1]
     chunks = 16 // math.gcd(16, rows)
     width = features // chunks
@@ -341,23 +393,23 @@
     group_rows = QUAD * block_rows
     group_slots = QUAD * rows
 
-    row = jnp.arange(group_rows)
+    row = np.arange(group_rows)
     slot = (row // block_rows) * rows + row % rows
-    rid = jnp.broadcast_to((row % block_rows // rows)[:, None], (group_rows, 2 * ff))
-    rid = rid.astype(jnp.float32)
-    unfold = (slot[:, None] == jnp.arange(group_slots)[None, :])
-    fold = unfold.T.astype(jnp.float32)
+    rid = np.broadcast_to((row % block_rows // rows)[:, None], (group_rows, 2 * ff))
+    rid = rid.astype(np.float32)
+    unfold = slot[:, None] == np.arange(group_slots)[None, :]
+    fold = unfold.T.astype(np.float32)
     unfold = unfold.astype(jnp.bfloat16)
-    slots = jnp.arange(group_slots)
-    spread = (slots[:, None] % rows == jnp.arange(128)[None, :]).astype(jnp.float32)
-    collect = (slots[None, :] // rows == jnp.arange(8)[:, None]).astype(jnp.float32)
+    slots = np.arange(group_slots)
+    spread = (slots[:, None] % rows == np.arange(128)[None, :]).astype(np.float32)
+    collect = (slots[None, :] // rows == np.arange(8)[:, None]).astype(np.float32)
 
     vmem = pl.BlockSpec(memory_space=pltpu.VMEM)
     anywhere = pl.BlockSpec(memory_space=pl.ANY)
     block = (block_rows, width)
-    sems = 2 * (depth * 6 + 2 * (depth - 1)) + 2 + depth - 1
+    sems = 2 * (depth * 6 + 2 * (depth - 1)) + 6 + 2 + depth - 1 + 2
     return pl.pallas_call(
-        functools.partial(layer_kernel, slices, chunks),
+        functools.partial(layer_kernel, slices, chunks, hop),
         out_shape=(
             jax.ShapeDtypeStruct(block, jnp.bfloat16),
             jax.ShapeDtypeStruct(block, jnp.bfloat16),
@@ -376,6 +428,8 @@
             pltpu.VMEM((2, depth) + block, jnp.bfloat16),
             pltpu.VMEM((2, depth) + block, jnp.bfloat16),
             pltpu.VMEM((2, depth) + block, jnp.bfloat16),
+            pltpu.VMEM((2,) + block, jnp.bfloat16),
+            pltpu.VMEM((2,) + block, jnp.bfloat16),
             pltpu.VMEM((group_rows, width), jnp.float32),
             pltpu.VMEM((3, depth, 8, 128), jnp.float32),
             pltpu.VMEM((1 + depth, depth, 8, 128), jnp.float32),
@@ -401,7 +455,8 @@
         wanted = jnp.where(inside, weight[...], 0.0)
         high = wanted.astype(jnp.bfloat16)
         rest = (wanted - high.astype(jnp.float32)).astype(jnp.bfloat16)
-        out[...] = (dot(high, block[...]) + dot(rest, block[...])).astype(jnp.bfloat16)
+        total = dot(jnp.concatenate([high, rest], axis=0), block[...])
+        out[...] = (total[: high.shape[0]] + total[high.shape[0] :]).astype(jnp.bfloat16)
 
 
 def mix(block_f, block_b, weight_f, weight_b, rows):
@@ -473,7 +528,7 @@
 
     block_f, block_b, dots = run_layer(
         tok_f, tok_b, gate_w[0], up_w[0], down_w[0], place_f, place_b,
-        by_group(gate_pre[0]), by_group(up_pre[0]), slices, rows,
+        by_group(gate_pre[0]), by_group(up_pre[0]), slices, rows, experts == 1,
     )
     me = lax.axis_index("expert") % slices
     mine = lax.dynamic_slice(dots, (me // QUAD, me % QUAD, 0), (1, 1, 128))
@@ -499,8 +554,9 @@
 
     weight_f = from_behind(weight_table(placing_f, weights_f), "section", 1)
     weight_b = from_behind(weight_table(placing_b, weights_b), "section", -1)
-    block_f = from_behind(block_f, "section", 1)
-    block_b = from_behind(block_b, "section", -1)
+    if experts > 1:
+        block_f = from_behind(block_f, "section", 1)
+        block_b = from_behind(block_b, "section", -1)
     next_act, prev_grad = mix(block_f, block_b, weight_f, weight_b, rows)
     return (next_act[None], prev_grad[None], gate_grad[None])
 

time: 128 us -> 122 us (0.953)
  other arithmetic: 5.13 us -> 2.42 us
  Pallas kernels: 117 us -> 115 us
  local copies, waits for them, and re-layouts: 4.29 us -> 2.8 us
    convert_element_type x5 -> x0, other arithmetic: 2.67 us -> none  [the longest x1 0.74 us: run_layer(): unfold = unfold.astype(jnp.bfloat16)]
    pallas_call x1, Pallas kernels: 111 us -> 109 us  [run_layer(): pl.pallas_call(functools.partial(layer_kernel, slices, chunks, hop), out_...]
  transfers between devices with their start and end apart: 4 -> 2, of which waited for: 0 -> 0; matrix products, arithmetic and copies ran while one was open for 6% -> 3% of each run, Pallas kernels for 87% -> 90%
where the time goes in v2:
time: 122 us; the launch traced here: 121 us
  Pallas kernels  115 us (94%)
  local copies, waits for them, and re-layouts  2.8 us (2%)
  other arithmetic  2.42 us (2%)
    pallas_call x1, Pallas kernels, run_layer(): pl.pallas_call(functools.partial(layer_kernel, slices, chunks, hop), out_...  109 us
    pallas_call x1, Pallas kernels, mix(): pl.pallas_call(functools.partial(mix_kernel, rows), out_shape=(shape, sha...  5.65 us
  transfers between devices with their start and end apart: 2, of which 0 were waited for; matrix products, arithmetic and copies ran while one was open for 3% of the time, Pallas kernels for 90%

profile of v2, /device:TPU:0, one launch (start us, length us, event | category | flops | bytes accessed | tf_op | source)
XLA Modules:
  0.0 121.3 jit_solution(17931234870935554718)
XLA Ops:
  0.6 0.7 select_reduce_fusion.2
  1.4 0.1 select_reduce_fusion
  1.5 0.1 copy.22
  1.6 0.6 collective-permute-start.1
  2.2 0.7 select_reduce_fusion.3
  2.9 0.1 select_reduce_fusion.1
  3.1 0.1 copy.21
  3.2 0.1 collective-permute-start
  3.3 0.6 tile.37.place_b
  4.0 0.6 tile.17.place_f
  4.6 109.0 %moe_layer.1 = (bf16[80,896]{1,0:T(8,128)(2,1)}, bf16[80,896]{1,0:T(8,128)(2,1)}, f32[4,8,128]{2,1,0:T(8,128)}) custom-call(bf16[128,7168]{1,0:T(8,128)(2,1)} %bitcast.15, bf16[128,7168]{1,0:T(8,128)(2,1)} %bitcast.16, bf16[7168,128]{1,0:T(8,128)(2,1)} %bitcast.17, bf16[7168,128]{1,0:T(8,128)(2,1)} %bitcast.18, bf16[128,7168]{1,0:T(8,128)(2,1)} %bitcast.19, ...), custom_call_target="tpu_custom_call" | custom-call | tf_op jit(solution)/shard_map/moe_layer/pallas_call | solution.py:411
  113.6 0.7 constant_dynamic-slice_fusion
  114.3 0.1 fusion.10
  114.4 0.6 broadcast_select_fusion
  115.0 0.0 collective-permute-done.1.weight_b
  115.0 0.0 copy-start
  115.0 0.0 collective-permute-done.weight_f
  115.0 0.0 copy-start.1
  115.0 0.6 copy-done
  115.6 0.0 copy-done.1
  115.7 5.7 %mix.1 = (bf16[128,7168]{1,0:T(8,128)(2,1)}, bf16[128,7168]{1,0:T(8,128)(2,1)}) custom-call(bf16[80,896]{1,0:T(8,128)(2,1)} %get-tuple-element.8.block_f, bf16[80,896]{1,0:T(8,128)(2,1)} %get-tuple-element.9.block_b, f32[128,80]{1,0:T(8,128)} %copy-done.1, f32[128,80]{1,0:T(8,128)} %copy-done), custom_call_target="tpu_custom_call" | custom-call | tf_op jit(solution)/shard_map/mix/pallas_call | solution.py:470
  (15 shorter events, 0.1 us)
Async XLA Ops:
  1.6 113.4 %collective-permute-start.1 = (f32[128,80]{1,0:T(8,128)S(1)}, f32[128,80]{1,0:T(8,128)S(1)}, u32[]{:S(2)}, u32[]{:S(2)}) collective-permute-start(f32[128,80]{1,0:T(8,128)S(1)} %copy.22), channel_id=1, source_target_pairs={{0,16},{16,0},{1,17},{17,1},{2,18},{18,2},{3,19},{19,3},{4,20},{20... | collective-permute-start | bytes 122888 | tf_op jit(solution)/shard_map/ppermute | solution.py:20
  3.2 111.8 %collective-permute-start = (f32[128,80]{1,0:T(8,128)S(1)}, f32[128,80]{1,0:T(8,128)S(1)}, u32[]{:S(2)}, u32[]{:S(2)}) collective-permute-start(f32[128,80]{1,0:T(8,128)S(1)} %copy.21), channel_id=1, source_target_pairs={{0,16},{16,0},{1,17},{17,1},{2,18},{18,2},{3,19},{19,3},{4,20},{20... | collective-permute-start | bytes 122888 | tf_op jit(solution)/shard_map/ppermute | solution.py:20
  115.0 0.6 copy-start
  115.0 0.7 copy-start.1
